TPU v7x, 32 devices: a whole 2x2x4 slice. The times are simulated.
32 devices in a mesh: dp: 4 (over y, core), ctx: 8 (over z, x).
Axes of the slice: x: 2, y: 2, z: 4, core: 2. Of those that a mesh axis runs over, the one named last changes fastest.
Arguments:
- text: bfloat16 [4, 2, 128, 2048], P('dp', None, None, 'ctx'), may hold values from -6 to 6
- src: int32 [4], replicated, may hold values from 0 to 3, each once
- lengths: int32 [4, 2], replicated, may hold values from 1 to 128
- kv_weight: bfloat16 [2048, 2, 8192], P('dp', None, 'ctx'), may hold values from -0.125 to 0.125
- queries: bfloat16 [4, 2048, 4096], P('dp', 'ctx'), may hold values from -160 to 160
- grad_out: bfloat16 [4, 2048, 4096], P('dp', 'ctx'), may hold values from -6 to 6
Outputs:
- attended: bfloat16 [4, 2048, 4096], P('dp', 'ctx')
- grad_queries: bfloat16 [4, 2048, 4096], P('dp', 'ctx')
- grad_weight: float32 [2048, 2, 8192], P('dp', None, 'ctx')
Inputs may be any that keep to these rules, and one draw needn't show every extreme that they name: `src`: each text sample is used by exactly one latent sample. `lengths`: tokens of an encoder output at or beyond its length are padding.
All inputs are finite; a program needn't handle non-finite values.
Results may differ from a plain program's by a relative error of at most 0.018.
The roundings to bfloat16 on the way count: a program that leaves them out, or rounds other values in their place, can miss the bound.
Values may be sent and summed in bfloat16 or wider, within the bound.
A program may use at most 128 MiB of HBM per device.

v0:
```python
import math
import jax
import jax.numpy as jnp
from jax import lax
from jax.sharding import PartitionSpec as P

HEAD = 128


def attend(queries, key_value, valid, grad_out):
    batch, length, width = queries.shape
    heads = width // HEAD
    keys = key_value.shape[1] * key_value.shape[2]
    scale = 1.0 / math.sqrt(HEAD)
    paired = key_value.reshape(batch, keys, heads, 2, HEAD)
    key = paired[:, :, :, 0]
    value = paired[:, :, :, 1]
    q_rows = queries.reshape(batch, length, heads, HEAD)
    g_rows = grad_out.reshape(batch, length, heads, HEAD)
    scores = jnp.einsum("blhd,bjhd->bhlj", q_rows, key, preferred_element_type=jnp.float32) * scale
    scores = jnp.where(valid[:, None, None, :], scores, -1e30)
    top = jnp.max(scores, axis=-1, keepdims=True)
    weights = jnp.exp(scores - top)
    probs = weights / jnp.sum(weights, axis=-1, keepdims=True)
    probs_low = probs.astype(jnp.bfloat16)
    attended = jnp.einsum("bhlj,bjhd->blhd", probs_low, value, preferred_element_type=jnp.float32)
    attended = attended.reshape(batch, length, width).astype(jnp.bfloat16)
    grad_probs = jnp.einsum("blhd,bjhd->bhlj", g_rows, value, preferred_element_type=jnp.float32)
    delta = jnp.sum(probs * grad_probs, axis=-1, keepdims=True)
    grad_scores = (probs * (grad_probs - delta) * scale).astype(jnp.bfloat16)
    grad_queries = jnp.einsum(
        "bhlj,bjhd->blhd", grad_scores, key, preferred_element_type=jnp.float32
    )
    grad_queries = grad_queries.reshape(batch, length, width).astype(jnp.bfloat16)
    grad_key = jnp.einsum(
        "bhlj,blhd->bjhd", grad_scores, q_rows, preferred_element_type=jnp.float32
    )
    grad_value = jnp.einsum(
        "bhlj,blhd->bjhd", probs_low, g_rows, preferred_element_type=jnp.float32
    )
    grad_kv = jnp.stack([grad_key, grad_value], axis=3).reshape(
        batch, 2, keys // 2, heads * 2 * HEAD
    )
    return (attended, grad_queries, grad_kv)


def per_device(text, src, lengths, kv_weight, queries, grad_out):
    per_group = queries.shape[0]
    group = lax.axis_index("dp")
    everyone = lax.all_gather(text, "dp", axis=0, tiled=True)
    chosen_ids = lax.dynamic_slice_in_dim(src, group * per_group, per_group, 0)
    picked = jnp.take(everyone, chosen_ids, axis=0)
    full_text = lax.all_gather(picked, "ctx", axis=3, tiled=True)
    tokens = full_text.shape[2]
    rows = full_text
    kv_local = jnp.einsum(
        "betf,fec->betc",
        rows,
        lax.all_gather(kv_weight, "dp", axis=0, tiled=True),
        preferred_element_type=jnp.float32,
    ).astype(jnp.bfloat16)
    chosen_lengths = jnp.take(lengths, chosen_ids, axis=0)
    positions = jnp.arange(tokens, dtype=jnp.int32)
    valid = (positions[None, None, :] < chosen_lengths[:, :, None]).reshape(per_group, 2 * tokens)
    moved_queries, moved_grads = (
        lax.all_to_all(queries, "ctx", split_axis=2, concat_axis=1, tiled=True),
        lax.all_to_all(grad_out, "ctx", split_axis=2, concat_axis=1, tiled=True),
    )
    head_out, head_grad, grad_kv = attend(moved_queries, kv_local, valid, moved_grads)
    attended, grad_queries = (
        lax.all_to_all(head_out, "ctx", split_axis=1, concat_axis=2, tiled=True),
        lax.all_to_all(head_grad, "ctx", split_axis=1, concat_axis=2, tiled=True),
    )
    grad_low = grad_kv.astype(jnp.bfloat16)
    rows = full_text
    grad_weight = lax.psum_scatter(
        jnp.einsum("betf,betc->fec", rows, grad_low, preferred_element_type=jnp.float32).astype(
            jnp.bfloat16
        ),
        "dp",
        scatter_dimension=0,
        tiled=True,
    ).astype(jnp.float32)
    return (attended, grad_queries, grad_weight)


def solution(mesh):
    placed = (
        P("dp", None, None, "ctx"),
        P(),
        P(),
        P("dp", None, "ctx"),
        P("dp", "ctx", None),
        P("dp", "ctx", None),
    )
    return jax.shard_map(
        per_device,
        mesh=mesh,
        in_specs=placed,
        out_specs=(P("dp", "ctx", None), P("dp", "ctx", None), P("dp", None, "ctx")),
        check_vma=False,
    )
```

profile of v0, /device:TPU:0, one launch (start us, length us, event | category | flops | bytes accessed | tf_op | source)
XLA Modules:
  0.0 400.6 jit_solution(18149222278047048982)
XLA Ops:
  7.2 1.4 dynamic_slice.3
  10.6 8.9 %all_gather.9 = bf16[4,2,128,256]{3,2,1,0:T(8,128)(2,1)S(1)} all-gather(bf16[1,2,128,256]{3,2,1,0:T(8,128)(2,1)} %param.6), channel_id=1, replica_groups=mesh['dp'=4,'ctx'=8] {'dp'}, dimensions={0}, use_global_device_ids=true | all-gather | bytes 655360 | tf_op jit(solution)/shard_map/all_gather | solution.py:50
  20.2 3.5 copy.79
  23.7 7.1 %copy.82 = bf16[1,256,4096]{1,0,2:T(2,128)(2,1)} copy(bf16[1,256,4096]{2,1,0:T(8,128)(2,1)S(1)} %copy-done.1) | data formatting | bytes 4194304 | tf_op args[4]
  31.3 21.5 %reduce.8 = bf16[4096,256]{1,0:T(8,128)(2,1)S(1)} reduce(bf16[4096,1,256]{2,1,0:T(2,128)(2,1)} %bitcast.142, bf16[]{:T(256)} %broadcast.122), dimensions={1}, to_apply=%bitcast.123.reduce_sub_computation | reduce | bytes 4194306
  52.8 3.2 reshape.226
  56.0 5.8 %all-to-all-start = ((bf16[8,2,65536]{2,1,0:T(2,128)(2,1)}), bf16[8,2,65536]{2,1,0:T(2,128)(2,1)S(1)}, u32[]{:S(2)}, u32[]{:S(2)}) async-start(bf16[8,2,65536]{2,1,0:T(2,128)(2,1)} %reshape.226), calls=%async_computation | async-start | bytes 4194304 | tf_op jit(solution)/shard_map/all_to_all | solution.py:66
  61.8 10.1 %copy.88 = bf16[1,256,4096]{1,0,2:T(2,128)(2,1)} copy(bf16[1,256,4096]{2,1,0:T(8,128)(2,1)} %param.11) | data formatting | bytes 4194304 | tf_op args[5]
  71.9 22.8 %reduce.10 = bf16[4096,256]{1,0:T(8,128)(2,1)} reduce(bf16[4096,1,256]{2,1,0:T(2,128)(2,1)} %bitcast.149, bf16[]{:T(256)} %broadcast.122), dimensions={1}, to_apply=%bitcast.121.reduce_sub_computation | reduce | bytes 4194306
  94.7 5.8 %reshape.224 = bf16[8,2,65536]{2,1,0:T(2,128)(2,1)} reshape(bf16[4096,256]{1,0:T(8,128)(2,1)} %reduce.10) | data formatting | bytes 4194304
  100.6 10.0 %all-to-all-done = bf16[8,2,65536]{2,1,0:T(2,128)(2,1)S(1)} async-done(((bf16[8,2,65536]{2,1,0:T(2,128)(2,1)}), bf16[8,2,65536]{2,1,0:T(2,128)(2,1)S(1)}, u32[]{:S(2)}, u32[]{:S(2)}) %all-to-all-start) | async-done | bytes 2097184 | tf_op jit(solution)/shard_map/all_to_all | solution.py:66
  110.5 4.4 %all-to-all-start.2 = ((bf16[8,2,65536]{2,1,0:T(2,128)(2,1)}), bf16[8,2,65536]{2,1,0:T(2,128)(2,1)}, u32[]{:S(2)}, u32[]{:S(2)}) async-start(bf16[8,2,65536]{2,1,0:T(2,128)(2,1)} %reshape.224), calls=%async_computation.2 | async-start | bytes 4194304 | tf_op jit(solution)/shard_map/all_to_all | solution.py:67
  115.5 4.3 %reshape.227 = bf16[4096,1,256]{2,1,0:T(2,128)(2,1)} reshape(bf16[8,2,65536]{2,1,0:T(2,128)(2,1)S(1)} %all-to-all-done) | data formatting | bytes 4194304
  119.8 2.5 copy.112
  123.6 2.3 reshape.172
  125.9 36.9 %all-to-all-done.2 = bf16[8,2,65536]{2,1,0:T(2,128)(2,1)} async-done(((bf16[8,2,65536]{2,1,0:T(2,128)(2,1)}), bf16[8,2,65536]{2,1,0:T(2,128)(2,1)}, u32[]{:S(2)}, u32[]{:S(2)}) %all-to-all-start.2) | async-done | bytes 2097184 | tf_op jit(solution)/shard_map/all_to_all | solution.py:67
  162.8 6.7 %reshape.225 = bf16[4096,1,256]{2,1,0:T(2,128)(2,1)} reshape(bf16[8,2,65536]{2,1,0:T(2,128)(2,1)} %all-to-all-done.2) | data formatting | bytes 4194304
  169.5 2.5 copy.114
  172.1 2.5 copy.89
  174.6 2.9 reshape.173
  177.5 5.0 %fusion.19 = bf16[1,2,128,1024]{3,2,1,0:T(8,128)(2,1)S(1)} fusion(bf16[2048,2,1024]{2,0,1:T(8,128)(2,1)} %all-gather.5.cloned.1.call-done, bf16[1,2,128,2048]{3,2,1,0:T(8,128)(2,1)} %all-gather.3.cloned.1.call-done), kind=kOutput, calls=%fused_computation.26 | convolution fusion | flops 1074003968 | bytes 9961472 | tf_op jit(solution)/shard_map/betf,fec->betc/dot_general | solution.py:56
  182.9 1.5 fusion.42
  185.4 4.5 %fusion.32 = f32[4,256,2048]{2,1,0:T(8,128)} fusion(bf16[2048,4,128]{0,2,1:T(8,128)(2,1)S(1)} %reshape.173, bf16[1,256,4,1,128]{1,4,2,3,0:T(8,128)(2,1)S(1)} %copy.116), kind=kOutput, calls=%fused_computation.36 | convolution fusion | flops 536870912 | bytes 10747904 | tf_op jit(solution)/shard_map/blhd,bjhd->bhlj/dot_general | solution.py:28
  189.9 8.0 %fusion.43 = (f32[4,2048]{1,0:T(4,128)S(1)}, f32[4,2048,256]{1,2,0:T(8,128)}) fusion(pred[256]{0:T(512)(128)(4,1)S(1)} %bitcast_compare_fusion, bf16[2048,4,128]{0,2,1:T(8,128)(2,1)} %reshape.172, bf16[1,256,4,1,128]{4,3,2,1,0:T(2,128)(2,1)S(1)} %copy-done.2), kind=kOutput, calls=%fused_computation.50 | convolution fusion | flops 545259776 | bytes 10780928 | tf_op jit(solution)/shard_map/sub | solution.py:23
  197.9 4.6 %fusion.24 = bf16[1,256,4,1,128]{4,1,2,3,0:T(8,128)(2,1)S(1)} fusion(bf16[2048,4,128]{0,2,1:T(8,128)(2,1)S(1)} %reshape.173, f32[4,2048,256]{1,2,0:T(8,128)} %get-tuple-element.43, f32[4,2048]{1,0:T(4,128)S(1)} %get-tuple-element.42), kind=kOutput, calls=%fused_computation.29 | convolution fusion | flops 541196288 | bytes 10780672 | tf_op jit(solution)/shard_map/bhlj,blhd->bjhd/dot_general | solution.py:38
  202.6 14.9 %fusion.27 = bf16[1,256,4,1,128]{4,1,2,3,0:T(8,128)(2,1)S(1)} fusion(bf16[2048,4,128]{0,2,1:T(8,128)(2,1)} %reshape.172, f32[4,256,2048]{2,1,0:T(8,128)} %fusion.32, f32[4,2048,256]{1,2,0:T(8,128)} %get-tuple-element.43, f32[4,2048]{1,0:T(4,128)S(1)} %get-tuple-element.42), kind=kOutput, calls=%fused_computation.30 | convolution fusion | flops 551690496 | bytes 19169280 | tf_op jit(solution)/shard_map/bhlj,blhd->bjhd/dot_general | solution.py:35
  218.4 5.6 %convert_bitcast_fusion = bf16[2048,2,1024]{0,2,1:T(8,128)(2,1)} fusion(bf16[2,128,1024]{2,1,0:T(8,128)(2,1)S(1)} %convert_element_type.90, bf16[1,2,128,2048]{3,2,1,0:T(8,128)(2,1)S(1)} %copy-done), kind=kOutput, calls=%fused_computation.11 | convolution fusion | flops 1077936128 | bytes 9961472 | tf_op jit(solution)/shard_map/betf,betc->fec/dot_general | solution.py:77
  224.0 18.2 %fusion.15 = bf16[4,128,2048]{2,1,0:T(8,128)(2,1)S(1)} fusion(f32[4,256,2048]{2,1,0:T(8,128)} %fusion.32, bf16[1,256,4,1,128]{4,3,2,1,0:T(2,128)(2,1)S(1)} %copy-done.2, f32[4,2048,256]{1,2,0:T(8,128)} %get-tuple-element.43, f32[4,2048]{1,0:T(4,128)S(1)} %get-tuple-element.42), kind=kOutput, calls=%fused_computation.20 | convolution fusion | flops 552608000 | bytes 19169280 | tf_op jit(solution)/shard_map/bhlj,bjhd->blhd/dot_general | solution.py:31
  242.3 7.5 %copy.94 = bf16[1,2048,512]{2,0,1:T(2,128)(2,1)} copy(bf16[1,2048,512]{1,2,0:T(8,128)(2,1)S(1)} %bitcast.157) | data formatting | bytes 4194304 | tf_op jit(solution)/shard_map/convert_element_type | solution.py:34
  249.8 14.0 %reduce.11 = bf16[2048,512]{1,0:T(8,128)(2,1)S(1)} reduce(bf16[2048,1,512]{2,1,0:T(2,128)(2,1)} %bitcast.146, bf16[]{:T(256)} %broadcast.122), dimensions={1}, to_apply=%bitcast.127.reduce_sub_computation | reduce | bytes 4194306
  263.8 3.8 reshape.230
  267.6 3.6 all-to-all-start.3
  271.2 5.7 %convolution_convert_fusion = bf16[4,128,2048]{2,1,0:T(8,128)(2,1)} fusion(bf16[1,256,4,1,128]{1,4,2,3,0:T(8,128)(2,1)S(1)} %copy.116, f32[4,2048,256]{1,2,0:T(8,128)} %get-tuple-element.43, f32[4,2048]{1,0:T(4,128)S(1)} %get-tuple-element.42), kind=kOutput, calls=%fused_computation.21 | convolution fusion | flops 542113792 | bytes 10780672 | tf_op jit(solution)/shard_map/bhlj,bjhd->blhd/dot_general | solution.py:26
  276.9 10.8 %copy.86 = bf16[1,2048,512]{2,0,1:T(2,128)(2,1)} copy(bf16[1,2048,512]{1,2,0:T(8,128)(2,1)} %bitcast.156) | data formatting | bytes 4194304 | tf_op jit(solution)/shard_map/convert_element_type | solution.py:27
  287.6 15.3 %reduce.9 = bf16[2048,512]{1,0:T(8,128)(2,1)} reduce(bf16[2048,1,512]{2,1,0:T(2,128)(2,1)} %bitcast.143, bf16[]{:T(256)} %broadcast.122), dimensions={1}, to_apply=%bitcast.125.reduce_sub_computation | reduce | bytes 4194306
  302.9 6.3 %reshape.228 = bf16[8,2,65536]{2,1,0:T(2,128)(2,1)} reshape(bf16[2048,512]{1,0:T(8,128)(2,1)} %reduce.9) | data formatting | bytes 4194304
  309.2 9.8 %all-to-all-done.3 = bf16[8,2,65536]{2,1,0:T(2,128)(2,1)S(1)} async-done(((bf16[8,2,65536]{2,1,0:T(2,128)(2,1)}), bf16[8,2,65536]{2,1,0:T(2,128)(2,1)S(1)}, u32[]{:S(2)}, u32[]{:S(2)}) %all-to-all-start.3) | async-done | bytes 2097184 | tf_op jit(solution)/shard_map/all_to_all | solution.py:72
  319.1 4.6 %all-to-all-start.1 = ((bf16[8,2,65536]{2,1,0:T(2,128)(2,1)}), bf16[8,2,65536]{2,1,0:T(2,128)(2,1)}, u32[]{:S(2)}, u32[]{:S(2)}) async-start(bf16[8,2,65536]{2,1,0:T(2,128)(2,1)} %reshape.228), calls=%async_computation.1 | async-start | bytes 4194304 | tf_op jit(solution)/shard_map/all_to_all | solution.py:71
  323.6 4.3 %reshape.231 = bf16[2048,1,512]{2,1,0:T(2,128)(2,1)} reshape(bf16[8,2,65536]{2,1,0:T(2,128)(2,1)S(1)} %all-to-all-done.3) | data formatting | bytes 4194304
  328.0 2.8 copy.115
  330.8 2.4 copy.95
  333.1 4.1 %copy.101 = bf16[1,256,4096]{2,1,0:T(8,128)(2,1)} copy(bf16[1,256,4096]{1,2,0:T(8,128)(2,1)} %bitcast.154) | data formatting | bytes 4194304
  337.2 34.2 %all-to-all-done.1 = bf16[8,2,65536]{2,1,0:T(2,128)(2,1)} async-done(((bf16[8,2,65536]{2,1,0:T(2,128)(2,1)}), bf16[8,2,65536]{2,1,0:T(2,128)(2,1)}, u32[]{:S(2)}, u32[]{:S(2)}) %all-to-all-start.1) | async-done | bytes 2097184 | tf_op jit(solution)/shard_map/all_to_all | solution.py:71
  371.4 6.7 %reshape.229 = bf16[2048,1,512]{2,1,0:T(2,128)(2,1)} reshape(bf16[8,2,65536]{2,1,0:T(2,128)(2,1)} %all-to-all-done.1) | data formatting | bytes 4194304
  378.2 2.8 copy.113
  381.0 2.4 copy.87
  383.3 4.1 %copy.100 = bf16[1,256,4096]{2,1,0:T(8,128)(2,1)} copy(bf16[1,256,4096]{1,2,0:T(8,128)(2,1)} %bitcast.155) | data formatting | bytes 4194304
  387.4 6.5 %copy.102 = f32[512,2,1024]{2,1,0:T(2,128)} copy(bf16[512,2,1024]{0,2,1:T(8,128)(2,1)} %reduce-scatter.2.cloned.1.call-done) | data formatting | bytes 6291456
  (28 shorter events, 5.4 us)
Async XLA Ops:
  7.2 16.6 %copy-start.1 = (bf16[1,256,4096]{2,1,0:T(8,128)(2,1)S(1)}, bf16[1,256,4096]{2,1,0:T(8,128)(2,1)}, u32[]{:S(2)}) copy-start(bf16[1,256,4096]{2,1,0:T(8,128)(2,1)} %param.10) | copy-start | bytes 6291460
  7.2 170.3 %all-gather.3.cloned.1.call-start = ((), (), s32[]{:S(2)}) async-start(), calls=%async_computation.5 | async-start | bytes 1179648 | tf_op jit(solution)/shard_map/all_gather | solution.py:53
  20.1 157.4 %all-gather.5.cloned.1.call-start = ((), (), s32[]{:S(2)}) async-start(), calls=%async_computation.6 | async-start | bytes 10485760 | tf_op jit(solution)/shard_map/all_gather | solution.py:59
  56.0 54.6 %all-to-all-start = ((bf16[8,2,65536]{2,1,0:T(2,128)(2,1)}), bf16[8,2,65536]{2,1,0:T(2,128)(2,1)S(1)}, u32[]{:S(2)}, u32[]{:S(2)}) async-start(bf16[8,2,65536]{2,1,0:T(2,128)(2,1)} %reshape.226), calls=%async_computation | async-start | bytes 4194304 | tf_op jit(solution)/shard_map/all_to_all | solution.py:66
  94.7 20.5 %copy-start.3 = (s32[4,2]{0,1:T(2,128)S(1)}, s32[4,2]{0,1:T(2,128)}, u32[]{:S(2)}) copy-start(s32[4,2]{0,1:T(2,128)} %param.8) | copy-start | bytes 100
  110.5 52.3 %all-to-all-start.2 = ((bf16[8,2,65536]{2,1,0:T(2,128)(2,1)}), bf16[8,2,65536]{2,1,0:T(2,128)(2,1)}, u32[]{:S(2)}, u32[]{:S(2)}) async-start(bf16[8,2,65536]{2,1,0:T(2,128)(2,1)} %reshape.224), calls=%async_computation.2 | async-start | bytes 4194304 | tf_op jit(solution)/shard_map/all_to_all | solution.py:67
  114.9 272.5 %reduce-scatter.2.cloned.1.call-start = ((), (), s32[]{:S(2)}) async-start(), calls=%async_computation.7 | async-start | bytes 10485760 | tf_op jit(solution)/shard_map/reduce_scatter | solution.py:76
  185.4 4.5 %copy-start.2 = (bf16[1,256,4,1,128]{4,3,2,1,0:T(2,128)(2,1)S(1)}, bf16[1,256,4,1,128]{4,3,2,1,0:T(2,128)(2,1)}, u32[]{:S(2)}) copy-start(bf16[1,256,4,1,128]{4,3,2,1,0:T(2,128)(2,1)} %get-tuple-element.40) | copy-start | bytes 786436
  202.5 15.9 %copy-start = (bf16[1,2,128,2048]{3,2,1,0:T(8,128)(2,1)S(1)}, bf16[1,2,128,2048]{3,2,1,0:T(8,128)(2,1)}, u32[]{:S(2)}) copy-start(bf16[1,2,128,2048]{3,2,1,0:T(8,128)(2,1)} %all-gather.3.cloned.1.call-done) | copy-start | bytes 3145732
  267.6 51.5 %all-to-all-start.3 = ((bf16[8,2,65536]{2,1,0:T(2,128)(2,1)}), bf16[8,2,65536]{2,1,0:T(2,128)(2,1)S(1)}, u32[]{:S(2)}, u32[]{:S(2)}) async-start(bf16[8,2,65536]{2,1,0:T(2,128)(2,1)} %reshape.230), calls=%async_computation.3 | async-start | bytes 4194304 | tf_op jit(solution)/shard_map/all_to_all | solution.py:72
  319.1 52.4 %all-to-all-start.1 = ((bf16[8,2,65536]{2,1,0:T(2,128)(2,1)}), bf16[8,2,65536]{2,1,0:T(2,128)(2,1)}, u32[]{:S(2)}, u32[]{:S(2)}) async-start(bf16[8,2,65536]{2,1,0:T(2,128)(2,1)} %reshape.228), calls=%async_computation.1 | async-start | bytes 4194304 | tf_op jit(solution)/shard_map/all_to_all | solution.py:71
Sparse Core Ops, SparseCore 0:
  20.3 40.1 all-gather.2
  62.6 57.2 all-gather.4
  224.2 69.8 reduce-scatter.1
where the time goes:
time: 409 us; the launch traced here: 401 us
  local copies, waits for them, and re-layouts  125 us (31%)
  waiting for transfers between devices  91 us (22%)
  other arithmetic  74.5 us (18%)
  matrix products  66.5 us (16%)
  starting transfers between devices  18.8 us (5%)
  between operations  16.1 us (4%)
  blocking collectives  8.89 us (2%)
    unnamed x28, local copies, waits for them, and re-layouts  88.7 us
    unnamed x4, other arithmetic  73.6 us
    all_to_all x1, waiting for transfers between devices, per_device(): lax.all_to_all(grad_out, 'ctx', split_axis=2, concat_axis=1, tiled=True)  36.9 us
    all_to_all x1, waiting for transfers between devices, per_device(): lax.all_to_all(head_out, 'ctx', split_axis=1, concat_axis=2, tiled=True)  34.2 us
    dot_general x1, matrix products, attend(): jnp.einsum('bhlj,bjhd->blhd', grad_scores, key, preferred_element_type=jn...  18.2 us
    dot_general x1, matrix products, attend(): jnp.einsum('bhlj,blhd->bjhd', grad_scores, q_rows, preferred_element_type...  14.9 us
    convert_element_type x1, local copies, waits for them, and re-layouts, attend(): attended = attended.reshape(batch, length, width).astype(jnp.bfloat16)  10.8 us
    all_to_all x1, waiting for transfers between devices, per_device(): lax.all_to_all(queries, 'ctx', split_axis=2, concat_axis=1, tiled=True)  9.97 us
  transfers between devices with their start and end apart: 7, of which 4 were waited for; matrix products, arithmetic and copies ran while one was open for 53% of the time, Pallas kernels for 0%

commit v1 on v0

--- a/solution.py
+++ b/solution.py
@@ -64,7 +64,12 @@
     valid = (positions[None, None, :] < chosen_lengths[:, :, None]).reshape(per_group, 2 * tokens)
     moved_queries, moved_grads = (
         lax.all_to_all(queries, "ctx", split_axis=2, concat_axis=1, tiled=True),
-        lax.all_to_all(grad_out, "ctx", split_axis=2, concat_axis=1, tiled=True),
+        jnp.concatenate(
+            lax.all_to_all(
+                jnp.stack(jnp.split(grad_out, lax.axis_size("ctx"), axis=2)), "ctx", 0, 0
+            ),
+            axis=1,
+        ),
     )
     head_out, head_grad, grad_kv = attend(moved_queries, kv_local, valid, moved_grads)
     attended, grad_queries = (

time: 409 us -> 387 us (0.946); the launches traced: 401 us -> 385 us
  other arithmetic: 74.5 us -> 51.7 us
  waiting for transfers between devices: 91 us -> 109 us
  local copies, waits for them, and re-layouts: 125 us -> 116 us
    all_to_all x1, waiting for transfers between devices: 9.97 us -> 39.7 us  [per_device(): lax.all_to_all(queries, 'ctx', split_axis=2, concat_axis=1, tiled=True)]
    unnamed x4 -> x3, other arithmetic: 73.6 us -> 50.8 us
    unnamed x28 -> x33, local copies, waits for them, and re-layouts: 88.7 us -> 75 us
    all_to_all x1, waiting for transfers between devices: 36.9 us -> 25 us  [per_device(): lax.all_to_all(jnp.stack(jnp.split(grad_out, lax.axis_size('ctx'), axis=2...]
    another operation x2 -> x4, local copies, waits for them, and re-layouts: 5.22 us -> 12.4 us
  transfers between devices with their start and end apart: 7 -> 7, of which waited for: 4 -> 4; matrix products, arithmetic and copies ran while one was open for 53% -> 47% of each run, Pallas kernels for 0% -> 0%
where the time goes in v1:
time: 387 us; the launch traced here: 385 us
  local copies, waits for them, and re-layouts  116 us (30%)
  waiting for transfers between devices  109 us (28%)
  matrix products  66.5 us (17%)
  other arithmetic  51.7 us (13%)
  starting transfers between devices  17.8 us (5%)
  between operations  15.9 us (4%)
  blocking collectives  8.89 us (2%)
    unnamed x33, local copies, waits for them, and re-layouts  75 us
    unnamed x3, other arithmetic  50.8 us
    all_to_all x1, waiting for transfers between devices, per_device(): lax.all_to_all(queries, 'ctx', split_axis=2, concat_axis=1, tiled=True)  39.7 us
    all_to_all x1, waiting for transfers between devices, per_device(): lax.all_to_all(head_out, 'ctx', split_axis=1, concat_axis=2, tiled=True)  34.1 us
    all_to_all x1, waiting for transfers between devices, per_device(): lax.all_to_all(jnp.stack(jnp.split(grad_out, lax.axis_size('ctx'), axis=2...  25 us
    dot_general x1, matrix products, attend(): jnp.einsum('bhlj,bjhd->blhd', grad_scores, key, preferred_element_type=jn...  18.2 us
    dot_general x1, matrix products, attend(): jnp.einsum('bhlj,blhd->bjhd', grad_scores, q_rows, preferred_element_type...  14.9 us
    convert_element_type x1, local copies, waits for them, and re-layouts, attend(): attended = attended.reshape(batch, length, width).astype(jnp.bfloat16)  10.8 us
  transfers between devices with their start and end apart: 7, of which 4 were waited for; matrix products, arithmetic and copies ran while one was open for 47% of the time, Pallas kernels for 0%

profile of v1, /device:TPU:0, one launch (start us, length us, event | category | flops | bytes accessed | tf_op | source)
XLA Modules:
  0.0 385.1 jit_solution(16305777681979383123)
XLA Ops:
  10.4 8.9 %all_gather.9 = bf16[4,2,128,256]{3,2,1,0:T(8,128)(2,1)S(1)} all-gather(bf16[1,2,128,256]{3,2,1,0:T(8,128)(2,1)} %param.6), channel_id=1, replica_groups=mesh['dp'=4,'ctx'=8] {'dp'}, dimensions={0}, use_global_device_ids=true | all-gather | bytes 655360 | tf_op jit(solution)/shard_map/all_gather | solution.py:50
  20.0 3.5 copy.83
  23.6 1.8 bitcast_dynamic-update-slice_fusion.7
  25.4 1.7 bitcast_dynamic-update-slice_fusion.6
  27.1 1.7 bitcast_dynamic-update-slice_fusion.5
  28.8 1.7 bitcast_dynamic-update-slice_fusion.4
  30.5 1.7 bitcast_dynamic-update-slice_fusion.3
  33.8 1.7 bitcast_dynamic-update-slice_fusion.1
  35.5 1.7 bitcast_dynamic-update-slice_fusion
  37.2 5.8 %all-to-all-start.2 = ((bf16[8,1,256,512]{3,2,1,0:T(8,128)(2,1)}), bf16[8,1,256,512]{3,2,1,0:T(8,128)(2,1)}, u32[]{:S(2)}, u32[]{:S(2)}) async-start(bf16[8,1,256,512]{3,2,1,0:T(8,128)(2,1)} %bitcast_dynamic-update-slice_fusion), calls=%async_computation.2 | async-start | bytes 4194304 | tf_op jit(solution)/shard_map/all_to_all | solution.py:68
  43.0 7.1 %copy.86 = bf16[1,256,4096]{1,0,2:T(2,128)(2,1)} copy(bf16[1,256,4096]{2,1,0:T(8,128)(2,1)S(1)} %copy-done.2) | data formatting | bytes 4194304 | tf_op args[4]
  50.5 21.5 %reduce.8 = bf16[4096,256]{1,0:T(8,128)(2,1)S(1)} reduce(bf16[4096,1,256]{2,1,0:T(2,128)(2,1)} %bitcast.117, bf16[]{:T(256)} %broadcast.122), dimensions={1}, to_apply=%bitcast.98.reduce_sub_computation | reduce | bytes 4194306
  72.0 3.2 reshape.223
  75.2 25.0 %all-to-all-done.2 = bf16[8,1,256,512]{3,2,1,0:T(8,128)(2,1)} async-done(((bf16[8,1,256,512]{3,2,1,0:T(8,128)(2,1)}), bf16[8,1,256,512]{3,2,1,0:T(8,128)(2,1)}, u32[]{:S(2)}, u32[]{:S(2)}) %all-to-all-start.2) | async-done | bytes 2097184 | tf_op jit(solution)/shard_map/all_to_all | solution.py:68
  100.2 3.6 all-to-all-start
  104.2 4.0 %reshape.221 = bf16[2048,4,128]{2,1,0:T(4,128)(2,1)} reshape(bf16[8,1,256,512]{3,2,1,0:T(8,128)(2,1)} %all-to-all-done.2) | data formatting | bytes 4194304 | tf_op jit(solution)/shard_map/reshape.25
  108.1 4.4 %copy.109 = bf16[2048,4,128]{0,2,1:T(8,128)(2,1)} copy(bf16[2048,4,128]{2,1,0:T(4,128)(2,1)} %reshape.221) | data formatting | bytes 4194304 | tf_op jit(solution)/shard_map/reshape.25
  112.5 39.7 %all-to-all-done = bf16[8,2,65536]{2,1,0:T(2,128)(2,1)S(1)} async-done(((bf16[8,2,65536]{2,1,0:T(2,128)(2,1)}), bf16[8,2,65536]{2,1,0:T(2,128)(2,1)S(1)}, u32[]{:S(2)}, u32[]{:S(2)}) %all-to-all-start) | async-done | bytes 2097184 | tf_op jit(solution)/shard_map/all_to_all | solution.py:66
  152.3 4.3 %reshape.224 = bf16[4096,1,256]{2,1,0:T(2,128)(2,1)} reshape(bf16[8,2,65536]{2,1,0:T(2,128)(2,1)S(1)} %all-to-all-done) | data formatting | bytes 4194304
  156.6 2.5 copy.120
  160.3 2.3 reshape.170
  162.7 5.0 %fusion.24 = bf16[1,2,128,1024]{3,2,1,0:T(8,128)(2,1)S(1)} fusion(bf16[2048,2,1024]{2,0,1:T(8,128)(2,1)} %all-gather.5.cloned.1.call-done, bf16[1,2,128,2048]{3,2,1,0:T(8,128)(2,1)} %all-gather.3.cloned.1.call-done), kind=kOutput, calls=%fused_computation.23 | convolution fusion | flops 1074003968 | bytes 9961472 | tf_op jit(solution)/shard_map/betf,fec->betc/dot_general | solution.py:56
  170.2 4.5 %fusion.41 = f32[4,2048,256]{1,2,0:T(8,128)} fusion(bf16[2048,4,128]{0,2,1:T(8,128)(2,1)S(1)} %copy-done.1, bf16[1,256,4,1,128]{1,4,2,3,0:T(8,128)(2,1)S(1)} %copy.123), kind=kOutput, calls=%fused_computation.41 | convolution fusion | flops 536870912 | bytes 10747904 | tf_op jit(solution)/shard_map/blhd,bjhd->bhlj/dot_general | solution.py:28
  174.7 8.0 %fusion.52 = (f32[4,2048]{1,0:T(4,128)S(1)}, f32[4,2048,256]{1,2,0:T(8,128)}) fusion(pred[256]{0:T(512)(128)(4,1)S(1)} %bitcast_compare_fusion, bf16[2048,4,128]{0,2,1:T(8,128)(2,1)} %reshape.170, bf16[1,256,4,1,128]{4,3,2,1,0:T(2,128)(2,1)S(1)} %copy-done.3), kind=kOutput, calls=%fused_computation.55 | convolution fusion | flops 545259776 | bytes 10780928 | tf_op jit(solution)/shard_map/sub | solution.py:23
  182.7 4.6 %fusion.31 = bf16[1,256,4,1,128]{4,1,2,3,0:T(8,128)(2,1)S(1)} fusion(bf16[2048,4,128]{0,2,1:T(8,128)(2,1)S(1)} %copy-done.1, f32[4,2048,256]{1,2,0:T(8,128)} %get-tuple-element.43, f32[4,2048]{1,0:T(4,128)S(1)} %get-tuple-element.42), kind=kOutput, calls=%fused_computation.26 | convolution fusion | flops 541196288 | bytes 10780672 | tf_op jit(solution)/shard_map/bhlj,blhd->bjhd/dot_general | solution.py:38
  187.4 14.9 %fusion.34 = bf16[1,256,4,1,128]{4,1,2,3,0:T(8,128)(2,1)S(1)} fusion(bf16[2048,4,128]{0,2,1:T(8,128)(2,1)} %reshape.170, f32[4,2048,256]{1,2,0:T(8,128)} %fusion.41, f32[4,2048,256]{1,2,0:T(8,128)} %get-tuple-element.43, f32[4,2048]{1,0:T(4,128)S(1)} %get-tuple-element.42), kind=kOutput, calls=%fused_computation.27 | convolution fusion | flops 551690496 | bytes 19169280 | tf_op jit(solution)/shard_map/bhlj,blhd->bjhd/dot_general | solution.py:35
  203.2 5.6 %convert_bitcast_fusion = bf16[2048,2,1024]{0,2,1:T(8,128)(2,1)} fusion(bf16[2,128,1024]{2,1,0:T(8,128)(2,1)S(1)} %convert_element_type.90, bf16[1,2,128,2048]{3,2,1,0:T(8,128)(2,1)S(1)} %copy-done), kind=kOutput, calls=%fused_computation.6 | convolution fusion | flops 1077936128 | bytes 9961472 | tf_op jit(solution)/shard_map/betf,betc->fec/dot_general | solution.py:82
  208.9 18.2 %fusion.18 = bf16[4,128,2048]{2,1,0:T(8,128)(2,1)S(1)} fusion(f32[4,2048,256]{1,2,0:T(8,128)} %fusion.41, bf16[1,256,4,1,128]{4,3,2,1,0:T(2,128)(2,1)S(1)} %copy-done.3, f32[4,2048,256]{1,2,0:T(8,128)} %get-tuple-element.43, f32[4,2048]{1,0:T(4,128)S(1)} %get-tuple-element.42), kind=kOutput, calls=%fused_computation.17 | convolution fusion | flops 552608000 | bytes 19169280 | tf_op jit(solution)/shard_map/bhlj,bjhd->blhd/dot_general | solution.py:31
  227.1 7.5 %copy.97 = bf16[1,2048,512]{2,0,1:T(2,128)(2,1)} copy(bf16[1,2048,512]{1,2,0:T(8,128)(2,1)S(1)} %bitcast.129) | data formatting | bytes 4194304 | tf_op jit(solution)/shard_map/convert_element_type | solution.py:34
  234.6 14.0 %reduce.10 = bf16[2048,512]{1,0:T(8,128)(2,1)S(1)} reduce(bf16[2048,1,512]{2,1,0:T(2,128)(2,1)} %bitcast.120, bf16[]{:T(256)} %broadcast.122), dimensions={1}, to_apply=%bitcast.102.reduce_sub_computation | reduce | bytes 4194306
  248.6 3.8 reshape.227
  252.4 3.6 all-to-all-start.3
  256.0 5.7 %convolution_convert_fusion = bf16[4,128,2048]{2,1,0:T(8,128)(2,1)} fusion(bf16[1,256,4,1,128]{1,4,2,3,0:T(8,128)(2,1)S(1)} %copy.123, f32[4,2048,256]{1,2,0:T(8,128)} %get-tuple-element.43, f32[4,2048]{1,0:T(4,128)S(1)} %get-tuple-element.42), kind=kOutput, calls=%fused_computation.18 | convolution fusion | flops 542113792 | bytes 10780672 | tf_op jit(solution)/shard_map/bhlj,bjhd->blhd/dot_general | solution.py:26
  261.7 10.8 %copy.90 = bf16[1,2048,512]{2,0,1:T(2,128)(2,1)} copy(bf16[1,2048,512]{1,2,0:T(8,128)(2,1)} %bitcast.128) | data formatting | bytes 4194304 | tf_op jit(solution)/shard_map/convert_element_type | solution.py:27
  272.5 15.3 %reduce.9 = bf16[2048,512]{1,0:T(8,128)(2,1)} reduce(bf16[2048,1,512]{2,1,0:T(2,128)(2,1)} %bitcast.118, bf16[]{:T(256)} %broadcast.122), dimensions={1}, to_apply=%bitcast.100.reduce_sub_computation | reduce | bytes 4194306
  287.8 6.3 %reshape.225 = bf16[8,2,65536]{2,1,0:T(2,128)(2,1)} reshape(bf16[2048,512]{1,0:T(8,128)(2,1)} %reduce.9) | data formatting | bytes 4194304
  294.1 9.8 %all-to-all-done.3 = bf16[8,2,65536]{2,1,0:T(2,128)(2,1)S(1)} async-done(((bf16[8,2,65536]{2,1,0:T(2,128)(2,1)}), bf16[8,2,65536]{2,1,0:T(2,128)(2,1)S(1)}, u32[]{:S(2)}, u32[]{:S(2)}) %all-to-all-start.3) | async-done | bytes 2097184 | tf_op jit(solution)/shard_map/all_to_all | solution.py:77
  303.8 4.6 %all-to-all-start.1 = ((bf16[8,2,65536]{2,1,0:T(2,128)(2,1)}), bf16[8,2,65536]{2,1,0:T(2,128)(2,1)}, u32[]{:S(2)}, u32[]{:S(2)}) async-start(bf16[8,2,65536]{2,1,0:T(2,128)(2,1)} %reshape.225), calls=%async_computation.1 | async-start | bytes 4194304 | tf_op jit(solution)/shard_map/all_to_all | solution.py:76
  308.5 4.3 %reshape.228 = bf16[2048,1,512]{2,1,0:T(2,128)(2,1)} reshape(bf16[8,2,65536]{2,1,0:T(2,128)(2,1)S(1)} %all-to-all-done.3) | data formatting | bytes 4194304
  312.8 2.8 copy.122
  315.6 2.4 copy.98
  318.0 4.1 %copy.105 = bf16[1,256,4096]{2,1,0:T(8,128)(2,1)} copy(bf16[1,256,4096]{1,2,0:T(8,128)(2,1)} %bitcast.126) | data formatting | bytes 4194304
  322.0 34.1 %all-to-all-done.1 = bf16[8,2,65536]{2,1,0:T(2,128)(2,1)} async-done(((bf16[8,2,65536]{2,1,0:T(2,128)(2,1)}), bf16[8,2,65536]{2,1,0:T(2,128)(2,1)}, u32[]{:S(2)}, u32[]{:S(2)}) %all-to-all-start.1) | async-done | bytes 2097184 | tf_op jit(solution)/shard_map/all_to_all | solution.py:76
  356.1 6.7 %reshape.226 = bf16[2048,1,512]{2,1,0:T(2,128)(2,1)} reshape(bf16[8,2,65536]{2,1,0:T(2,128)(2,1)} %all-to-all-done.1) | data formatting | bytes 4194304
  362.9 2.8 copy.121
  365.7 2.4 copy.91
  368.0 4.1 %copy.104 = bf16[1,256,4096]{2,1,0:T(8,128)(2,1)} copy(bf16[1,256,4096]{1,2,0:T(8,128)(2,1)} %bitcast.127) | data formatting | bytes 4194304
  372.1 6.5 %copy.106 = f32[512,2,1024]{2,1,0:T(2,128)} copy(bf16[512,2,1024]{0,2,1:T(8,128)(2,1)} %reduce-scatter.2.cloned.1.call-done) | data formatting | bytes 6291456
  (33 shorter events, 9.2 us)
Async XLA Ops:
  7.2 155.5 %all-gather.3.cloned.1.call-start = ((), (), s32[]{:S(2)}) async-start(), calls=%async_computation.5 | async-start | bytes 1179648 | tf_op jit(solution)/shard_map/all_gather | solution.py:53
  20.0 142.7 %all-gather.5.cloned.1.call-start = ((), (), s32[]{:S(2)}) async-start(), calls=%async_computation.6 | async-start | bytes 10485760 | tf_op jit(solution)/shard_map/all_gather | solution.py:59
  23.6 19.4 %copy-start.2 = (bf16[1,256,4096]{2,1,0:T(8,128)(2,1)S(1)}, bf16[1,256,4096]{2,1,0:T(8,128)(2,1)}, u32[]{:S(2)}) copy-start(bf16[1,256,4096]{2,1,0:T(8,128)(2,1)} %param.10) | copy-start | bytes 6291460
  37.2 63.1 %all-to-all-start.2 = ((bf16[8,1,256,512]{3,2,1,0:T(8,128)(2,1)}), bf16[8,1,256,512]{3,2,1,0:T(8,128)(2,1)}, u32[]{:S(2)}, u32[]{:S(2)}) async-start(bf16[8,1,256,512]{3,2,1,0:T(8,128)(2,1)} %bitcast_dynamic-update-slice_fusion), calls=%async_computation.2 | async-start | bytes 4194304 | tf_op jit(solution)/shard_map/all_to_all | solution.py:68
  72.0 31.9 %copy-start.4 = (s32[4,2]{0,1:T(2,128)S(1)}, s32[4,2]{0,1:T(2,128)}, u32[]{:S(2)}) copy-start(s32[4,2]{0,1:T(2,128)} %param.8) | copy-start | bytes 100
  100.2 52.0 %all-to-all-start = ((bf16[8,2,65536]{2,1,0:T(2,128)(2,1)}), bf16[8,2,65536]{2,1,0:T(2,128)(2,1)S(1)}, u32[]{:S(2)}, u32[]{:S(2)}) async-start(bf16[8,2,65536]{2,1,0:T(2,128)(2,1)} %reshape.223), calls=%async_computation | async-start | bytes 4194304 | tf_op jit(solution)/shard_map/all_to_all | solution.py:66
  103.9 268.3 %reduce-scatter.2.cloned.1.call-start = ((), (), s32[]{:S(2)}) async-start(), calls=%async_computation.7 | async-start | bytes 10485760 | tf_op jit(solution)/shard_map/reduce_scatter | solution.py:81
  167.6 2.6 copy-start.1
  170.2 4.5 %copy-start.3 = (bf16[1,256,4,1,128]{4,3,2,1,0:T(2,128)(2,1)S(1)}, bf16[1,256,4,1,128]{4,3,2,1,0:T(2,128)(2,1)}, u32[]{:S(2)}) copy-start(bf16[1,256,4,1,128]{4,3,2,1,0:T(2,128)(2,1)} %get-tuple-element.40) | copy-start | bytes 786436
  187.4 15.9 %copy-start = (bf16[1,2,128,2048]{3,2,1,0:T(8,128)(2,1)S(1)}, bf16[1,2,128,2048]{3,2,1,0:T(8,128)(2,1)}, u32[]{:S(2)}) copy-start(bf16[1,2,128,2048]{3,2,1,0:T(8,128)(2,1)} %all-gather.3.cloned.1.call-done) | copy-start | bytes 3145732
  252.4 51.4 %all-to-all-start.3 = ((bf16[8,2,65536]{2,1,0:T(2,128)(2,1)}), bf16[8,2,65536]{2,1,0:T(2,128)(2,1)S(1)}, u32[]{:S(2)}, u32[]{:S(2)}) async-start(bf16[8,2,65536]{2,1,0:T(2,128)(2,1)} %reshape.227), calls=%async_computation.3 | async-start | bytes 4194304 | tf_op jit(solution)/shard_map/all_to_all | solution.py:77
  303.8 52.3 %all-to-all-start.1 = ((bf16[8,2,65536]{2,1,0:T(2,128)(2,1)}), bf16[8,2,65536]{2,1,0:T(2,128)(2,1)}, u32[]{:S(2)}, u32[]{:S(2)}) async-start(bf16[8,2,65536]{2,1,0:T(2,128)(2,1)} %reshape.225), calls=%async_computation.1 | async-start | bytes 4194304 | tf_op jit(solution)/shard_map/all_to_all | solution.py:76
Sparse Core Ops, SparseCore 0:
  20.1 51.1 all-gather.2
  73.4 65.7 all-gather.4
  209.0 69.8 reduce-scatter.1
